TPU v7x, 256 devices: a whole 4x4x8 slice. The times are simulated.
256 devices in a mesh: gx: 16 (over z, core), gy: 16 (over x, y).
Axes of the slice: x: 4, y: 4, z: 8, core: 2. Of those that a mesh axis runs over, the one named last changes fastest.
Arguments:
- tokens: bfloat16 [4096, 4096], P('gx', 'gy'), may hold values from -6 to 6
- gate_blocks: bfloat16 [16, 16, 10, 128, 128], P('gy', 'gx'), may hold values from -0.125 to 0.125
- up_blocks: bfloat16 [16, 16, 10, 128, 128], P('gy', 'gx'), may hold values from -0.125 to 0.125
- gate_coords: int32 [16, 16, 10, 2], P('gy', 'gx'), may hold values from 0 to 6, as said below
- gate_count: int32 [16, 16], P('gy', 'gx'), may hold values from 3 to 10, as said below
- down_blocks: bfloat16 [16, 16, 6, 128, 128], P('gx', 'gy'), may hold values from -0.09375 to 0.09375
- down_rows: int32 [16, 16, 4], P('gx'), may hold values from 0 to 6, as said below
- down_coords: int32 [16, 16, 6, 2], P('gx', 'gy'), may hold values from 0 to 3, as said below
- down_count: int32 [16, 16], P('gx', 'gy'), may hold values from 2 to 6, as said below
Outputs:
- mixed: bfloat16 [4096, 4096], P('gx', 'gy')
Inputs may be any that keep to these rules, and one draw needn't show every extreme that they name: `gate_coords`: within each tile the 10 (model-width block, hidden block) pairs are distinct, the first below 2, the second below 7; only the first gate_count slots are live. `gate_count`: some tile has all 10 slots live. `down_rows`: within each down tile the 4 hidden blocks are distinct. `down_coords`: within each down tile the 6 (kept-row index below 4, model-width block below 2) pairs are distinct; only the first down_count slots are live. `down_count`: some tile has all 6 slots live.
All inputs are finite; a program needn't handle non-finite values.
Results may differ from a plain program's by a relative error of at most 0.025.
Values may be sent and summed in bfloat16 or wider, within the bound.
A program may use at most 64 MiB of HBM per device.

v0:
```python
import jax
import jax.numpy as jnp
from jax import lax
from jax.sharding import PartitionSpec as P

FF = 14336
BLOCK = 128


def cut_along(value, dim, count):
    shape = value.shape
    parts = value.reshape(*shape[:dim], count, shape[dim] // count, *shape[dim + 1 :])
    return jnp.moveaxis(parts, dim, 0)


def piece_ends(length, count):
    hop = length // count
    if hop >= 8:
        hop -= hop % 8
    return [hop * k for k in range(1, count)]


def in_order(parts, dim):
    parts = jnp.moveaxis(parts, 0, dim)
    shape = parts.shape
    return parts.reshape(*shape[:dim], shape[dim] * shape[dim + 1], *shape[dim + 2 :])


def cut_exchange(value, axis, pieces, split_dim, concat_dim):
    parts = cut_along(value, split_dim, lax.axis_size(axis))
    split_at = max(range(1, max(2, parts.ndim - 1)), key=lambda d: parts.shape[d])
    done = []
    for section in jnp.split(parts, piece_ends(parts.shape[split_at], pieces), axis=split_at):
        if section.size:
            done.append(lax.all_to_all(section, axis, split_axis=0, concat_axis=0, tiled=True))
    return in_order(jnp.concatenate(done, axis=split_at), concat_dim)


def tile_dense(blocks, coords, count, row_count, col_count):
    live = (jnp.arange(coords.shape[0]) < count).astype(jnp.bfloat16)
    pick = jax.nn.one_hot(coords[:, 0], row_count, dtype=jnp.bfloat16)
    place = jax.nn.one_hot(coords[:, 1], col_count, dtype=jnp.bfloat16) * live[:, None]
    dense = jnp.einsum(
        "sr,sc,skm->rkcm", pick, place, blocks, preferred_element_type=jnp.float32
    ).astype(jnp.bfloat16)
    return dense.reshape(row_count * blocks.shape[1], col_count * blocks.shape[2])


def body(
    tokens,
    gate_blocks,
    up_blocks,
    gate_coords,
    gate_count,
    down_blocks,
    down_rows,
    down_coords,
    down_count,
):
    n_model = tokens.shape[1] // BLOCK
    n_hidden = FF // (BLOCK * lax.axis_size("gx"))
    paired_blocks = jnp.concatenate([gate_blocks[:, 0], up_blocks[:, 0]], -1)
    gathered = lax.all_gather(tokens, "gx", axis=0, tiled=True)
    tok_rows = gathered.shape[0] // lax.axis_size("gy")
    dense_pair = tile_dense(
        paired_blocks[0], gate_coords[0, 0], gate_count[0, 0], n_model, n_hidden
    )
    summed = lax.psum_scatter(
        jnp.dot(gathered, dense_pair, preferred_element_type=jnp.float32).astype(jnp.bfloat16),
        "gy",
        scatter_dimension=0,
        tiled=True,
    ).astype(jnp.float32)
    summed = summed.reshape(tok_rows, n_hidden, 2, BLOCK)
    hidden = (jax.nn.silu(summed[:, :, 0]) * summed[:, :, 1]).astype(jnp.bfloat16)
    kept_count = down_rows.shape[-1]
    dense_down = tile_dense(
        down_blocks[0, 0], down_coords[0, 0], down_count[0, 0], kept_count, n_model
    )
    select_every = jax.nn.one_hot(down_rows[0], n_hidden, dtype=jnp.bfloat16)
    outgoing = jnp.einsum(
        "nfk,guf->gnuk", hidden, select_every, preferred_element_type=jnp.float32
    ).astype(jnp.bfloat16)
    outgoing = outgoing.reshape(outgoing.shape[0], tok_rows, kept_count * BLOCK)
    received = cut_exchange(outgoing, "gy", 2, 0, 0)
    kept_all = received.reshape(received.shape[0] * tok_rows, kept_count * BLOCK)
    partial_out = jnp.dot(kept_all, dense_down, preferred_element_type=jnp.float32)
    return lax.psum_scatter(partial_out.astype(jnp.bfloat16), "gx", scatter_dimension=0, tiled=True)


def solution(mesh):
    return jax.shard_map(
        body,
        mesh=mesh,
        in_specs=(
            P("gx", "gy"),
            P("gy", "gx", None, None, None),
            P("gy", "gx", None, None, None),
            P("gy", "gx", None, None),
            P("gy", "gx"),
            P("gx", "gy", None, None, None),
            P("gx", None, None),
            P("gx", "gy", None, None),
            P("gx", "gy"),
        ),
        out_specs=P("gx", "gy"),
        check_vma=False,
    )
```

profile of v0, /device:TPU:2, one launch (start us, length us, event | category | flops | bytes accessed | tf_op | source)
XLA Modules:
  0.0 320.3 jit_solution(4454195248453779331)
XLA Ops:
  6.5 0.0 all-gather.2.cloned.1.call-start
  6.5 0.7 all-gather.2.cloned.1.call-update
  7.3 0.0 reduce-scatter.3.cloned.1.call-start
  8.0 0.8 slice_bitcast_fusion.5
  8.7 1.5 copy_bitcast_fusion
  10.3 0.4 convolution_convert_fusion.2
  10.7 0.3 copy.50
  11.0 40.6 %all-gather.2.cloned.1.call-done = bf16[4096,256]{1,0:T(8,128)(2,1)} async-done(((bf16[256,256]{1,0:T(8,128)(2,1)}), bf16[4096,256]{1,0:T(8,128)(2,1)}) %all-gather.2.cloned.1.call-update) | async-done | bytes 2097168 | tf_op jit(solution)/shard_map/all_gather | solution.py:63
  51.6 8.9 %fusion = bf16[4096,1792]{0,1:T(8,128)(2,1)} fusion(bf16[256,1792]{1,0:T(8,128)(2,1)S(1)} %bitcast.95, bf16[4096,256]{1,0:T(8,128)(2,1)} %all-gather.2.cloned.1.call-done), kind=kOutput, calls=%fused_computation.1 | convolution fusion | flops 3765436416 | bytes 17694720 | tf_op jit(solution)/shard_map/dot_general | solution.py:69
  60.5 0.0 reduce-scatter.3.cloned.1.call-update
  60.5 105.2 %reduce-scatter.3.cloned.1.call-done = bf16[256,1792]{0,1:T(8,128)(2,1)} async-done(((bf16[4096,1792]{0,1:T(8,128)(2,1)}), bf16[256,1792]{0,1:T(8,128)(2,1)}) %reduce-scatter.3.cloned.1.call-update) | async-done | bytes 917520 | tf_op jit(solution)/shard_map/reduce_scatter | solution.py:68
  165.7 1.3 fusion.31
  167.1 0.0 copy-start.1
  167.1 0.4 copy.48
  167.5 0.4 copy.49
  167.9 0.0 copy-done.1
  167.9 3.0 convert_bitcast_fusion
  170.9 7.5 %copy.37 = bf16[16,256,4,128]{1,3,2,0:T(8,128)(2,1)} copy(bf16[16,256,4,128]{3,0,1,2:T(8,128)(2,1)} %convert_bitcast_fusion) | data formatting | bytes 8388608 | tf_op jit(solution)/shard_map/convert_element_type | solution.py:83
  178.4 4.0 %slice_bitcast_fusion.1 = (bf16[16,1,128,512]{2,3,1,0:T(8,128)(2,1)S(1)}, bf16[16,1,128,512]{2,3,1,0:T(8,128)(2,1)}) fusion(bf16[16,1,256,512]{2,3,0,1:T(8,128)(2,1)} %bitcast.94), kind=kLoop, calls=%fused_computation.6 | loop fusion | bytes 8388608 | tf_op jit(solution)/shard_map/split | solution.py:33
  182.4 31.4 %all_to_all.10 = bf16[16,1,128,512]{2,3,1,0:T(8,128)(2,1)} all-to-all(bf16[16,1,128,512]{2,3,1,0:T(8,128)(2,1)S(1)} %get-tuple-element.5), channel_id=1, replica_groups=mesh['gx'=16,'gy'=16] {'gy'}, dimensions={0} | all-to-all | bytes 4194304 | tf_op jit(solution)/shard_map/all_to_all | solution.py:35
  213.8 0.0 copy-start.2
  213.8 0.0 copy-start
  213.8 6.0 %all-to-all-start.1 = ((bf16[16,1,128,512]{2,3,1,0:T(8,128)(2,1)}), bf16[16,1,128,512]{2,3,1,0:T(8,128)(2,1)S(1)}, u32[]{:S(2)}, u32[]{:S(2)}) async-start(bf16[16,1,128,512]{2,3,1,0:T(8,128)(2,1)} %get-tuple-element.6), calls=%async_computation.2 | async-start | bytes 4194304 | tf_op jit(solution)/shard_map/all_to_all | solution.py:35
  219.8 0.0 reduce-scatter.5.cloned.1.call-start
  220.5 0.0 copy-done.2
  220.5 0.0 copy-done
  220.5 0.2 fusion.1
  220.8 0.3 copy.43
  221.1 3.9 %copy.40 = bf16[16,1,128,512]{3,2,0,1:T(8,128)(2,1)} copy(bf16[16,1,128,512]{2,3,1,0:T(8,128)(2,1)} %all_to_all.10) | data formatting | bytes 4194304 | tf_op jit(solution)/shard_map/all_to_all | solution.py:35
  225.0 20.5 %all-to-all-done.1 = bf16[16,1,128,512]{2,3,1,0:T(8,128)(2,1)S(1)} async-done(((bf16[16,1,128,512]{2,3,1,0:T(8,128)(2,1)}), bf16[16,1,128,512]{2,3,1,0:T(8,128)(2,1)S(1)}, u32[]{:S(2)}, u32[]{:S(2)}) %all-to-all-start.1) | async-done | bytes 2097184 | tf_op jit(solution)/shard_map/all_to_all | solution.py:35
  245.4 2.6 copy.41
  248.0 2.6 pad_maximum_fusion
  250.6 2.6 convolution_convert_fusion.1
  253.2 0.0 reduce-scatter.5.cloned.1.call-update
  253.2 60.6 %reduce-scatter.5.cloned.1.call-done = bf16[256,256]{1,0:T(8,128)(2,1)} async-done(((bf16[4096,256]{1,0:T(8,128)(2,1)}), bf16[256,256]{1,0:T(8,128)(2,1)}) %reduce-scatter.5.cloned.1.call-update) | async-done | bytes 131088 | tf_op jit(solution)/shard_map/reduce_scatter | solution.py:88
  (7 shorter events, 0.0 us)
Async XLA Ops:
  6.5 45.1 %all-gather.2.cloned.1.call-start = ((), (), s32[]{:S(2)}) async-start(), calls=%async_computation.4 | async-start | bytes 2228224 | tf_op jit(solution)/shard_map/all_gather | solution.py:63
  7.3 158.5 %reduce-scatter.3.cloned.1.call-start = ((), (), s32[]{:S(2)}) async-start(), calls=%async_computation.5 | async-start | bytes 15597568 | tf_op jit(solution)/shard_map/reduce_scatter | solution.py:68
  167.1 0.8 copy-start.1
  213.8 6.7 %copy-start.2 = (s32[1,1,6,2]{2,3,1,0:T(2,128)S(1)}, s32[1,1,6,2]{2,3,1,0:T(2,128)}, u32[]{:S(2)}) copy-start(s32[1,1,6,2]{2,3,1,0:T(2,128)} %param.16) | copy-start | bytes 148
  213.8 6.7 %copy-start = (bf16[1,1,6,128,128]{4,3,2,1,0:T(8,128)(2,1)S(1)}, bf16[1,1,6,128,128]{4,3,2,1,0:T(8,128)(2,1)}, u32[]{:S(2)}) copy-start(bf16[1,1,6,128,128]{4,3,2,1,0:T(8,128)(2,1)} %param.14) | copy-start | bytes 589828
  213.8 31.6 %all-to-all-start.1 = ((bf16[16,1,128,512]{2,3,1,0:T(8,128)(2,1)}), bf16[16,1,128,512]{2,3,1,0:T(8,128)(2,1)S(1)}, u32[]{:S(2)}, u32[]{:S(2)}) async-start(bf16[16,1,128,512]{2,3,1,0:T(8,128)(2,1)} %get-tuple-element.6), calls=%async_computation.2 | async-start | bytes 4194304 | tf_op jit(solution)/shard_map/all_to_all | solution.py:35
  219.8 94.0 %reduce-scatter.5.cloned.1.call-start = ((), (), s32[]{:S(2)}) async-start(), calls=%async_computation.6 | async-start | bytes 2228224 | tf_op jit(solution)/shard_map/reduce_scatter | solution.py:88
Sparse Core Ops, SparseCore 0:
  9.2 42.3 all-gather.1
  60.6 105.0 reduce-scatter.2
  253.3 60.4 reduce-scatter.4
where the time goes:
time: 321 us; the launch traced here: 320 us
  waiting for transfers between devices  228 us (71%)
  blocking collectives  31.4 us (10%)
  local copies, waits for them, and re-layouts  23 us (7%)
  matrix products  15.1 us (5%)
  between operations  14.5 us (5%)
  starting transfers between devices  6.04 us (2%)
    reduce_scatter x1, waiting for transfers between devices, body(): lax.psum_scatter(jnp.dot(gathered, dense_pair, preferred_element_type=jnp...  105 us
    reduce_scatter x1, waiting for transfers between devices, body(): lax.psum_scatter(partial_out.astype(jnp.bfloat16), 'gx', scatter_dimensio...  60.6 us
    all_gather x1, waiting for transfers between devices, body(): gathered = lax.all_gather(tokens, 'gx', axis=0, tiled=True)  40.6 us
    all_to_all x1, blocking collectives, cut_exchange(): lax.all_to_all(section, axis, split_axis=0, concat_axis=0, tiled=True)  31.4 us
    all_to_all x1, waiting for transfers between devices, cut_exchange(): lax.all_to_all(section, axis, split_axis=0, concat_axis=0, tiled=True)  20.5 us
    dot_general x1, matrix products, body(): jnp.dot(gathered, dense_pair, preferred_element_type=jnp.float32)  8.91 us
    convert_element_type x1, local copies, waits for them, and re-layouts, body(): outgoing = jnp.einsum('nfk,guf->gnuk', hidden, select_every, preferred_el...  7.47 us
    all_to_all x2, local copies, waits for them, and re-layouts, cut_exchange(): lax.all_to_all(section, axis, split_axis=0, concat_axis=0, tiled=True)  6.51 us
  transfers between devices with their start and end apart: 4, of which 4 were waited for; matrix products, arithmetic and copies ran while one was open for 2% of the time, Pallas kernels for 0%

commit v1 on v0

--- a/solution.py
+++ b/solution.py
@@ -5,6 +5,18 @@
 
 FF = 14336
 BLOCK = 128
+
+
+def collect(x, axis, dim):
+    ways, here, step = (lax.axis_size(axis), lax.axis_index(axis), x.shape[dim])
+    line, have = (x, 1)
+    while have < ways:
+        line = jnp.concatenate(
+            [line, lax.ppermute(line, axis, [(d, (d - have) % ways) for d in range(ways)])],
+            axis=dim,
+        )
+        have = 2 * have
+    return jnp.roll(line, here * step, axis=dim)
 
 
 def cut_along(value, dim, count):
@@ -60,7 +72,7 @@
     n_model = tokens.shape[1] // BLOCK
     n_hidden = FF // (BLOCK * lax.axis_size("gx"))
     paired_blocks = jnp.concatenate([gate_blocks[:, 0], up_blocks[:, 0]], -1)
-    gathered = lax.all_gather(tokens, "gx", axis=0, tiled=True)
+    gathered = collect(tokens, "gx", 0)
     tok_rows = gathered.shape[0] // lax.axis_size("gy")
     dense_pair = tile_dense(
         paired_blocks[0], gate_coords[0, 0], gate_count[0, 0], n_model, n_hidden

time: 321 us -> 378 us (1.18)
  waiting for transfers between devices: 228 us -> 263 us
  starting transfers between devices: 6.04 us -> 19.4 us
  other arithmetic: 2.61 us -> 6.42 us
  local copies, waits for them, and re-layouts: 23 us -> 26.8 us
    ppermute x0 -> x4, waiting for transfers between devices: none -> 73.6 us  [collect(): lax.ppermute(line, axis, [(d, (d - have) % ways) for d in range(ways)])]
    all_gather x1 -> x0, waiting for transfers between devices: 40.6 us -> none  [body(): gathered = lax.all_gather(tokens, 'gx', axis=0, tiled=True)]
    ppermute x0 -> x4, starting transfers between devices: none -> 13.3 us  [collect(): lax.ppermute(line, axis, [(d, (d - have) % ways) for d in range(ways)])]
    concatenate x0 -> x3, other arithmetic: none -> 3.81 us  [collect(): jnp.concatenate([line, lax.ppermute(line, axis, [(d, (d - have) % ways) f...]
  transfers between devices with their start and end apart: 4 -> 7, of which waited for: 4 -> 7; matrix products, arithmetic and copies ran while one was open for 2% -> 2% of each run, Pallas kernels for 0% -> 0%
where the time goes in v1:
time: 378 us; the launch traced here: 377 us
  waiting for transfers between devices  263 us (70%)
  blocking collectives  31.6 us (8%)
  local copies, waits for them, and re-layouts  26.8 us (7%)
  starting transfers between devices  19.4 us (5%)
  matrix products  15.6 us (4%)
  between operations  14.9 us (4%)
  other arithmetic  6.42 us (2%)
    reduce_scatter x1, waiting for transfers between devices, body(): lax.psum_scatter(jnp.dot(gathered, dense_pair, preferred_element_type=jnp...  108 us
    ppermute x4, waiting for transfers between devices, collect(): lax.ppermute(line, axis, [(d, (d - have) % ways) for d in range(ways)])  73.6 us
    reduce_scatter x1, waiting for transfers between devices, body(): lax.psum_scatter(partial_out.astype(jnp.bfloat16), 'gx', scatter_dimensio...  60.4 us
    all_to_all x1, blocking collectives, cut_exchange(): lax.all_to_all(section, axis, split_axis=0, concat_axis=0, tiled=True)  31.6 us
    all_to_all x1, waiting for transfers between devices, cut_exchange(): lax.all_to_all(section, axis, split_axis=0, concat_axis=0, tiled=True)  20.4 us
    ppermute x4, starting transfers between devices, collect(): lax.ppermute(line, axis, [(d, (d - have) % ways) for d in range(ways)])  13.3 us
    dot_general x1, matrix products, body(): jnp.dot(gathered, dense_pair, preferred_element_type=jnp.float32)  9.32 us
  transfers between devices with their start and end apart: 7, of which 7 were waited for; matrix products, arithmetic and copies ran while one was open for 2% of the time, Pallas kernels for 0%

profile of v1, /device:TPU:2, one launch (start us, length us, event | category | flops | bytes accessed | tf_op | source)
XLA Modules:
  0.0 377.3 jit_solution(14268128567473515918)
XLA Ops:
  6.5 0.0 reduce-scatter.3.cloned.1.call-start
  6.5 5.3 %collective-permute-start = (bf16[256,256]{1,0:T(8,128)(2,1)}, bf16[256,256]{1,0:T(8,128)(2,1)S(1)}, u32[]{:S(2)}, u32[]{:S(2)}) collective-permute-start(bf16[256,256]{1,0:T(8,128)(2,1)} %param.9), channel_id=1, source_target_pairs={{0,240},{16,0},{32,16},{48,32},{64,48},{80,64},{96,80},{112,96},{1... | collective-permute-start | bytes 393224 | tf_op jit(solution)/shard_map/ppermute | solution.py:15
  11.8 2.8 collective-permute-done
  14.7 0.9 pad_maximum_fusion.3
  15.6 1.1 collective-permute-start.1
  17.3 4.7 %collective-permute-done.1 = bf16[512,256]{1,0:T(8,128)(2,1)S(1)} collective-permute-done((bf16[512,256]{1,0:T(8,128)(2,1)S(1)}, bf16[512,256]{1,0:T(8,128)(2,1)S(1)}, u32[]{:S(2)}, u32[]{:S(2)}) %collective-permute-start.1) | collective-permute-done | bytes 262176 | tf_op jit(solution)/shard_map/ppermute | solution.py:15
  22.0 0.9 pad_maximum_fusion.2
  23.0 0.0 copy-start
  23.0 3.7 collective-permute-start.2
  26.7 0.8 slice_bitcast_fusion.5
  27.4 19.7 %collective-permute-done.2 = bf16[1024,256]{1,0:T(8,128)(2,1)S(1)} collective-permute-done((bf16[1024,256]{1,0:T(8,128)(2,1)S(1)}, bf16[1024,256]{1,0:T(8,128)(2,1)S(1)}, u32[]{:S(2)}, u32[]{:S(2)}) %collective-permute-start.2) | collective-permute-done | bytes 524320 | tf_op jit(solution)/shard_map/ppermute | solution.py:15
  47.1 1.9 pad_maximum_fusion.1
  49.1 3.3 collective-permute-start.3
  52.4 1.5 copy_bitcast_fusion.2
  53.9 0.4 convolution_convert_fusion.2
  54.4 0.3 copy.50
  54.6 0.0 copy-done
  54.8 46.4 %collective-permute-done.3 = bf16[2048,256]{1,0:T(8,128)(2,1)S(1)} collective-permute-done((bf16[2048,256]{1,0:T(8,128)(2,1)}, bf16[2048,256]{1,0:T(8,128)(2,1)S(1)}, u32[]{:S(2)}, u32[]{:S(2)}) %collective-permute-start.3) | collective-permute-done | bytes 1048608 | tf_op jit(solution)/shard_map/ppermute | solution.py:15
  101.1 0.1 constant_dynamic-update-slice_fusion.5
  101.3 0.1 constant_dynamic-update-slice_fusion
  101.4 0.0 copy-start.1
  101.4 1.9 copy-done.1
  103.3 9.3 %convolution_convert_fusion = bf16[4096,1792]{1,0:T(8,128)(2,1)} fusion(bf16[256,1792]{1,0:T(8,128)(2,1)S(1)} %bitcast.97, bf16[8192,256]{1,0:T(8,128)(2,1)} %copy-done.1, s32[]{:T(128)S(6)} %select_n.14), kind=kOutput, calls=%fused_computation | convolution fusion | flops 3765436416 | bytes 17694724 | tf_op jit(solution)/shard_map/dot_general | solution.py:81
  112.7 0.0 reduce-scatter.3.cloned.1.call-update
  112.7 0.0 copy-start.3
  112.7 108.2 %reduce-scatter.3.cloned.1.call-done = bf16[256,1792]{1,0:T(8,128)(2,1)} async-done(((bf16[4096,1792]{1,0:T(8,128)(2,1)}), bf16[256,1792]{1,0:T(8,128)(2,1)}) %reduce-scatter.3.cloned.1.call-update) | async-done | bytes 917520 | tf_op jit(solution)/shard_map/reduce_scatter | solution.py:80
  220.9 2.2 reshape.29
  223.1 1.4 fusion.35
  224.5 0.0 copy-done.3
  224.5 3.0 convert_bitcast_fusion
  227.5 7.5 %copy.37 = bf16[16,256,4,128]{1,3,2,0:T(8,128)(2,1)} copy(bf16[16,256,4,128]{3,0,1,2:T(8,128)(2,1)} %convert_bitcast_fusion) | data formatting | bytes 8388608 | tf_op jit(solution)/shard_map/convert_element_type | solution.py:95
  235.0 4.0 %slice_bitcast_fusion.1 = (bf16[16,1,128,512]{2,3,1,0:T(8,128)(2,1)S(1)}, bf16[16,1,128,512]{2,3,1,0:T(8,128)(2,1)}) fusion(bf16[16,1,256,512]{2,3,0,1:T(8,128)(2,1)} %bitcast.94), kind=kLoop, calls=%fused_computation.5 | loop fusion | bytes 8388608 | tf_op jit(solution)/shard_map/split | solution.py:45
  239.0 0.0 copy-start.4
  239.0 0.0 copy-start.2
  239.0 31.6 %all_to_all.10 = bf16[16,1,128,512]{2,3,1,0:T(8,128)(2,1)} all-to-all(bf16[16,1,128,512]{2,3,1,0:T(8,128)(2,1)S(1)} %get-tuple-element.5), channel_id=1, replica_groups=mesh['gx'=16,'gy'=16] {'gy'}, dimensions={0} | all-to-all | bytes 4194304 | tf_op jit(solution)/shard_map/all_to_all | solution.py:47
  270.6 5.8 %all-to-all-start.1 = ((bf16[16,1,128,512]{2,3,1,0:T(8,128)(2,1)}), bf16[16,1,128,512]{2,3,1,0:T(8,128)(2,1)S(1)}, u32[]{:S(2)}, u32[]{:S(2)}) async-start(bf16[16,1,128,512]{2,3,1,0:T(8,128)(2,1)} %get-tuple-element.6), calls=%async_computation.2 | async-start | bytes 4194304 | tf_op jit(solution)/shard_map/all_to_all | solution.py:47
  276.4 0.2 reduce-scatter.5.cloned.1.call-start
  277.3 0.0 copy-done.4
  277.4 0.0 copy-done.2
  277.4 0.2 fusion.1
  277.6 0.3 copy.43
  277.9 3.9 %copy.40 = bf16[16,1,128,512]{3,2,0,1:T(8,128)(2,1)} copy(bf16[16,1,128,512]{2,3,1,0:T(8,128)(2,1)} %all_to_all.10) | data formatting | bytes 4194304 | tf_op jit(solution)/shard_map/all_to_all | solution.py:47
  281.9 20.4 %all-to-all-done.1 = bf16[16,1,128,512]{2,3,1,0:T(8,128)(2,1)S(1)} async-done(((bf16[16,1,128,512]{2,3,1,0:T(8,128)(2,1)}), bf16[16,1,128,512]{2,3,1,0:T(8,128)(2,1)S(1)}, u32[]{:S(2)}, u32[]{:S(2)}) %all-to-all-start.1) | async-done | bytes 2097184 | tf_op jit(solution)/shard_map/all_to_all | solution.py:47
  302.2 2.6 copy.41
  304.8 2.6 pad_maximum_fusion
  307.4 2.6 convolution_convert_fusion.1
  310.0 0.0 reduce-scatter.5.cloned.1.call-update
  310.0 60.4 %reduce-scatter.5.cloned.1.call-done = bf16[256,256]{1,0:T(8,128)(2,1)} async-done(((bf16[4096,256]{1,0:T(8,128)(2,1)}), bf16[256,256]{1,0:T(8,128)(2,1)}) %reduce-scatter.5.cloned.1.call-update) | async-done | bytes 131088 | tf_op jit(solution)/shard_map/reduce_scatter | solution.py:100
  (15 shorter events, 0.2 us)
Async XLA Ops:
  6.5 214.4 %reduce-scatter.3.cloned.1.call-start = ((), (), s32[]{:S(2)}) async-start(), calls=%async_computation.4 | async-start | bytes 15597568 | tf_op jit(solution)/shard_map/reduce_scatter | solution.py:80
  6.5 8.1 %collective-permute-start = (bf16[256,256]{1,0:T(8,128)(2,1)}, bf16[256,256]{1,0:T(8,128)(2,1)S(1)}, u32[]{:S(2)}, u32[]{:S(2)}) collective-permute-start(bf16[256,256]{1,0:T(8,128)(2,1)} %param.9), channel_id=1, source_target_pairs={{0,240},{16,0},{32,16},{48,32},{64,48},{80,64},{96,80},{112,96},{1... | collective-permute-start | bytes 393224 | tf_op jit(solution)/shard_map/ppermute | solution.py:15
  15.6 6.5 %collective-permute-start.1 = (bf16[512,256]{1,0:T(8,128)(2,1)S(1)}, bf16[512,256]{1,0:T(8,128)(2,1)S(1)}, u32[]{:S(2)}, u32[]{:S(2)}) collective-permute-start(bf16[512,256]{1,0:T(8,128)(2,1)S(1)} %pad_maximum_fusion.3), channel_id=1, source_target_pairs={{0,224},{16,240},{32,0},{48,16},{64,32},{80,48},{96,64},{112,80},{... | collective-permute-start | bytes 786440 | tf_op jit(solution)/shard_map/ppermute | solution.py:15
  23.0 31.6 %copy-start = (bf16[256,256]{1,0:T(8,128)(2,1)S(1)}, bf16[256,256]{1,0:T(8,128)(2,1)}, u32[]{:S(2)}) copy-start(bf16[256,256]{1,0:T(8,128)(2,1)} %param.9) | copy-start | bytes 393220
  23.0 24.1 %collective-permute-start.2 = (bf16[1024,256]{1,0:T(8,128)(2,1)S(1)}, bf16[1024,256]{1,0:T(8,128)(2,1)S(1)}, u32[]{:S(2)}, u32[]{:S(2)}) collective-permute-start(bf16[1024,256]{1,0:T(8,128)(2,1)S(1)} %pad_maximum_fusion.2), channel_id=1, source_target_pairs={{0,192},{16,208},{32,224},{48,240},{64,0},{80,16},{96,32},{112,48}... | collective-permute-start | bytes 1572872 | tf_op jit(solution)/shard_map/ppermute | solution.py:15
  49.1 52.0 %collective-permute-start.3 = (bf16[2048,256]{1,0:T(8,128)(2,1)}, bf16[2048,256]{1,0:T(8,128)(2,1)S(1)}, u32[]{:S(2)}, u32[]{:S(2)}) collective-permute-start(bf16[2048,256]{1,0:T(8,128)(2,1)} %pad_maximum_fusion.1), channel_id=1, source_target_pairs={{0,128},{16,144},{32,160},{48,176},{64,192},{80,208},{96,224},{112... | collective-permute-start | bytes 3145736 | tf_op jit(solution)/shard_map/ppermute | solution.py:15
  101.4 2.0 copy-start.1
  112.7 111.8 %copy-start.3 = (s32[1,16,4]{1,2,0:T(4,128)S(1)}, s32[1,16,4]{1,2,0:T(4,128)}, u32[]{:S(2)}) copy-start(s32[1,16,4]{1,2,0:T(4,128)} %param.15) | copy-start | bytes 772
  239.0 38.3 %copy-start.4 = (s32[1,1,6,2]{2,3,1,0:T(2,128)S(1)}, s32[1,1,6,2]{2,3,1,0:T(2,128)}, u32[]{:S(2)}) copy-start(s32[1,1,6,2]{2,3,1,0:T(2,128)} %param.16) | copy-start | bytes 148
  239.0 38.4 %copy-start.2 = (bf16[1,1,6,128,128]{4,3,2,1,0:T(8,128)(2,1)S(1)}, bf16[1,1,6,128,128]{4,3,2,1,0:T(8,128)(2,1)}, u32[]{:S(2)}) copy-start(bf16[1,1,6,128,128]{4,3,2,1,0:T(8,128)(2,1)} %param.14) | copy-start | bytes 589828
  270.6 31.6 %all-to-all-start.1 = ((bf16[16,1,128,512]{2,3,1,0:T(8,128)(2,1)}), bf16[16,1,128,512]{2,3,1,0:T(8,128)(2,1)S(1)}, u32[]{:S(2)}, u32[]{:S(2)}) async-start(bf16[16,1,128,512]{2,3,1,0:T(8,128)(2,1)} %get-tuple-element.6), calls=%async_computation.2 | async-start | bytes 4194304 | tf_op jit(solution)/shard_map/all_to_all | solution.py:47
  276.4 94.0 %reduce-scatter.5.cloned.1.call-start = ((), (), s32[]{:S(2)}) async-start(), calls=%async_computation.5 | async-start | bytes 2228224 | tf_op jit(solution)/shard_map/reduce_scatter | solution.py:100
Sparse Core Ops, SparseCore 0:
  112.8 108.0 reduce-scatter.2
  310.2 60.2 reduce-scatter.4
